TPU v7x, 32 devices: a whole 2x2x4 slice. The times are simulated.
32 devices in a mesh: tm: 8 (over y, x, core), func: 4 (over z).
Axes of the slice: x: 2, y: 2, z: 4, core: 2. Of those that a mesh axis runs over, the one named last changes fastest.
Arguments:
- initial_values: float32 [512, 1024], P('func'), may hold values from -6 to 6
- sensor_columns: int32 [128], replicated, may hold values from 0 to 1023
- space_cells: int32 [4096], P('tm'), may hold values from 0 to 1023
- time_cells: int32 [4096], P('tm'), may hold values from 0 to 63
- trunk_head: float32 [2, 256], replicated, may hold values from -8 to 8
- trunk_layers: float32 [3, 256, 256], replicated, may hold values from -0.375 to 0.375
- trunk_shifts: float32 [4, 256], replicated, may hold values from -3 to 3
- branch_head: float32 [128, 256], replicated, may hold values from -0.5 to 0.5
- branch_layers: float32 [4, 256, 256], replicated, may hold values from -0.375 to 0.375
- branch_shifts: float32 [5, 256], replicated, may hold values from -3 to 3
Outputs:
- total_loss: float32 [1], replicated
- trunk_head_gradient: float32 [2, 256], replicated
- trunk_layers_gradient: float32 [3, 256, 256], replicated
- trunk_shifts_gradient: float32 [4, 256], replicated
- branch_head_gradient: float32 [128, 256], replicated
- branch_layers_gradient: float32 [4, 256, 256], replicated
- branch_shifts_gradient: float32 [5, 256], replicated
All inputs are finite; a program needn't handle non-finite values.
Results may differ from a plain program's by a relative error of at most 0.00012.
Values sent between devices are 32-bit elements; how exact they have to be, the bound alone decides.
A program may use at most 128 MiB of HBM per device.

v0:
```python
import functools
import math

import jax
import jax.numpy as jnp
from jax import lax
from jax.experimental import pallas as pl
from jax.experimental.pallas import tpu as pltpu
from jax.sharding import PartitionSpec as P

SLAB_DEV = 4
GRID_T = 64


viscosity = 0.01 / math.pi
causal_rate = 3.0
epsilon = 1e-06
vmem_limit = 60 * 1024 * 1024


MESH_ID = pl.DeviceIdType.MESH


def factors_of(size):
    found = []
    for base in (4, 2, 3, 5, 7):
        while size % base == 0 and size > 1:
            found.append(base)
            size //= base
    return found + ([size] if size > 1 else [])


def digit_phases(tm_size, func_size):
    phases, stride, left = [], 1, tm_size
    while left % 2 == 0 and left > 1:
        phases.append(("tm", stride, 2))
        stride, left = stride * 2, left // 2
    if left > 1:
        phases.append(("tm", stride, left))
    stride = 1
    for size in factors_of(func_size):
        phases.append(("func", stride, size))
        stride *= size
    return phases


def digits_here(tm_size, func_size):
    tm_rank, func_rank = lax.axis_index("tm"), lax.axis_index("func")
    found = []
    phases = digit_phases(tm_size, func_size)
    swap = len(phases) >= 3 and all(phases[k][0] == "tm" and phases[k][2] == 2 for k in range(3))
    for spot, (axis, stride, size) in enumerate(phases):
        rank = tm_rank if axis == "tm" else func_rank
        if swap and spot in (1, 2):
            core = lax.rem(tm_rank, 2)
            other = phases[3 - spot][1]
            stride = (1 - core) * stride + core * other
            digit = lax.rem(rank // phases[spot][1], 2) * (1 - core) + lax.rem(rank // other, 2) * core
        else:
            digit = lax.rem(rank // stride, size)

        def peer_of(step, axis=axis, stride=stride, size=size, digit=digit, rank=rank):
            target = lax.rem(digit + step, size)
            place = rank + (target - digit) * stride
            return target, ((place, func_rank) if axis == "tm" else (tm_rank, place))

        found.append((size, digit, peer_of))
    return found


def split(value):
    high = value.astype(jnp.bfloat16)
    return high, (value - high.astype(jnp.float32)).astype(jnp.bfloat16)


def product(left, right, left_dim, right_dim):
    def once(a, b):
        return lax.dot_general(
            a, b, (((left_dim,), (right_dim,)), ((), ())), preferred_element_type=jnp.float32
        )

    return once(left[0], right[0]) + (once(left[0], right[1]) + once(left[1], right[0]))


def column_sum(value):
    return jnp.sum(value, axis=0, keepdims=True)


def terms_kernel(
    factor,
    start_factor,
    initial_ref,
    target_ref,
    column_ref,
    place_ref,
    start_ref,
    head_ref,
    layers_ref,
    shifts_ref,
    branch_head_ref,
    branch_layers_ref,
    branch_shifts_ref,
    terms_ref,
    energy_ref,
    layer_high,
    layer_low,
    branch_high,
    branch_low,
    hidden_high,
    hidden_low,
    value_keep,
    inner_keep,
    branch_keep,
    branch_keep_high,
    branch_keep_low,
    sensor_high,
    sensor_low,
    feature_high,
    feature_low,
):
    depth, breadth = layers_ref.shape[0], layers_ref.shape[2]
    branch_depth = branch_layers_ref.shape[0]
    sensors_count = branch_head_ref.shape[0]
    slab_rows = place_ref.shape[0] // SLAB_DEV
    start_rows = start_ref.shape[0]
    inverse_root = 1.0 / math.sqrt(breadth)
    small = (depth + branch_depth) * breadth + sensors_count
    terms_ref[:, small:, :] = jnp.zeros((terms_ref.shape[0], terms_ref.shape[1] - small, breadth), jnp.float32)
    for layer in range(depth):
        layer_high[layer], layer_low[layer] = split(layers_ref[layer])
    for layer in range(branch_depth):
        branch_high[layer], branch_low[layer] = split(branch_layers_ref[layer])

    grid = initial_ref.shape[1]
    picks = lax.broadcasted_iota(jnp.int32, (grid, sensors_count), 0) == column_ref[...]
    picks = picks.astype(jnp.float32).astype(jnp.bfloat16)
    left = initial_ref[...]
    sensors = jnp.zeros((left.shape[0], sensors_count), jnp.float32)
    for piece in range(3):
        part = left.astype(jnp.bfloat16)
        left = left - part.astype(jnp.float32)
        sensors = sensors + jnp.dot(part, picks, preferred_element_type=jnp.float32)
    pair = split(sensors)
    sensor_high[...], sensor_low[...] = pair
    hidden = jnp.tanh(product(pair, split(branch_head_ref[...]), 1, 0) + branch_shifts_ref[0:1, :])
    for layer in range(branch_depth):
        pair = split(hidden)
        branch_keep[layer] = hidden
        branch_keep_high[layer], branch_keep_low[layer] = pair
        hidden = product(pair, (branch_high[layer], branch_low[layer]), 1, 0)
        hidden = hidden + branch_shifts_ref[layer + 1 : layer + 2, :]
        if layer < branch_depth - 1:
            hidden = jnp.tanh(hidden)
    feature_high[...], feature_low[...] = split(hidden)

    space_row, time_row = head_ref[0:1, :], head_ref[1:2, :]

    def trunk(places, rows, streams):
        total = rows * streams
        values = jnp.tanh(places[:, 0:1] * space_row + places[:, 1:2] * time_row + shifts_ref[0:1, :])
        parts = [values]
        if streams > 1:
            slopes = 1.0 - values * values
            along = slopes * space_row
            parts += [along, slopes * time_row, -2.0 * values * along * space_row]
        for layer in range(depth):
            value_keep[layer, :rows] = parts[0]
            for stream, part in enumerate(parts):
                high, low = split(part)
                hidden_high[layer, stream * rows : (stream + 1) * rows] = high
                hidden_low[layer, stream * rows : (stream + 1) * rows] = low
            inner = product(
                (hidden_high[layer, :total], hidden_low[layer, :total]),
                (layer_high[layer], layer_low[layer]),
                1,
                0,
            )
            parts = [inner[stream * rows : (stream + 1) * rows] for stream in range(streams)]
            parts[0] = parts[0] + shifts_ref[layer + 1 : layer + 2, :]
            if layer == depth - 1:
                break
            values = jnp.tanh(parts[0])
            if streams > 1:
                inner_keep[layer, :total] = inner
                slopes = 1.0 - values * values
                along = slopes * parts[1]
                parts = [
                    values,
                    along,
                    slopes * parts[2],
                    slopes * parts[3] - 2.0 * values * along * parts[1],
                ]
            else:
                parts = [values]
        for stream, part in enumerate(parts):
            high, low = split(part)
            hidden_high[depth, stream * rows : (stream + 1) * rows] = high
            hidden_low[depth, stream * rows : (stream + 1) * rows] = low

    def trunk_back(group, places, rows, streams, adjoint):
        total = rows * streams
        for layer in reversed(range(depth)):
            pair = split(adjoint)
            terms_ref[group, layer * breadth : (layer + 1) * breadth, :] = product(
                (hidden_high[layer, :total], hidden_low[layer, :total]), pair, 0, 0
            )
            terms_ref[group, small + 2 + layer + 1 : small + 2 + layer + 2, :] = column_sum(adjoint[:rows])
            outer = product(pair, (layer_high[layer], layer_low[layer]), 1, 1)
            values = value_keep[layer, :rows]
            slopes = 1.0 - values * values
            if streams > 1:
                over_value, over_space, over_time, over_second = (
                    outer[stream * rows : (stream + 1) * rows] for stream in range(streams)
                )
                if layer > 0:
                    space, time, second = (
                        inner_keep[layer - 1, stream * rows : (stream + 1) * rows]
                        for stream in range(1, streams)
                    )
                    bend = second - 2.0 * values * space * space
                else:
                    space, time = space_row, time_row
                    bend = -2.0 * values * space * space
                over_slope = space * over_space + time * over_time + bend * over_second
                over_value = (
                    over_value
                    - 2.0 * values * over_slope
                    - 2.0 * slopes * space * space * over_second
                )
                over_space = slopes * over_space - 4.0 * values * slopes * space * over_second
                adjoint = jnp.concatenate(
                    [slopes * over_value, over_space, slopes * over_time, slopes * over_second], axis=0
                )
            else:
                adjoint = slopes * outer
        over_value = adjoint[:rows]
        space_sum = places[:, 0:1] * over_value
        time_sum = places[:, 1:2] * over_value
        if streams > 1:
            space_sum = space_sum + adjoint[rows : 2 * rows]
            time_sum = time_sum + adjoint[2 * rows : 3 * rows]
        terms_ref[group, small : small + 1, :] = column_sum(space_sum)
        terms_ref[group, small + 1 : small + 2, :] = column_sum(time_sum)
        terms_ref[group, small + 2 : small + 3, :] = column_sum(over_value)

    def branch_back(group, adjoint):
        place = small + 2 + depth + 1
        for layer in reversed(range(branch_depth)):
            pair = split(adjoint)
            begin = (depth + layer) * breadth
            terms_ref[group, begin : begin + breadth, :] = product(
                (branch_keep_high[layer], branch_keep_low[layer]), pair, 0, 0
            )
            terms_ref[group, place + layer + 1 : place + layer + 2, :] = column_sum(adjoint)
            hidden = branch_keep[layer]
            adjoint = product(pair, (branch_high[layer], branch_low[layer]), 1, 1)
            adjoint = (1.0 - hidden * hidden) * adjoint
        terms_ref[group, small - sensors_count : small, :] = product(
            (sensor_high[...], sensor_low[...]), split(adjoint), 0, 0
        )
        terms_ref[group, place : place + 1, :] = column_sum(adjoint)

    def whole_sum(value):
        total = jnp.sum(jnp.sum(value, axis=0, keepdims=True), axis=1, keepdims=True)
        return jnp.broadcast_to(total, (1, 128))

    def slab(group, carry):
        rows = slab_rows
        places = place_ref[pl.ds(pl.multiple_of(group * rows, 8), rows), :]
        trunk(places, rows, 4)
        features = (feature_high[...], feature_low[...])
        basis = (hidden_high[depth], hidden_low[depth])
        fields = product(features, basis, 1, 1) * inverse_root
        field, field_x, field_t, field_xx = (
            fields[:, stream * rows : (stream + 1) * rows] for stream in range(4)
        )
        residual = field_t + field * field_x - viscosity * field_xx
        energy_ref[pl.ds(group, 1), :] = whole_sum(residual * residual)
        scaled = (factor * inverse_root) * residual
        pair = split(
            jnp.concatenate([scaled * field_x, scaled * field, scaled, -viscosity * scaled], axis=1)
        )
        branch_back(group, product(pair, basis, 1, 0))
        trunk_back(group, places, rows, 4, product(pair, features, 0, 0))
        return carry

    lax.fori_loop(0, SLAB_DEV, slab, 0)
    rows = start_rows
    places = start_ref[...]
    trunk(places, rows, 1)
    features = (feature_high[...], feature_low[...])
    basis = (hidden_high[depth, :rows], hidden_low[depth, :rows])
    error = product(features, basis, 1, 1) * inverse_root - target_ref[...]
    energy_ref[SLAB_DEV:, :] = jnp.broadcast_to(whole_sum(error * error), (8 - SLAB_DEV, 128))
    pair = split((start_factor * inverse_root) * error)
    branch_back(SLAB_DEV, product(pair, basis, 1, 0))
    trunk_back(SLAB_DEV, places, rows, 1, product(pair, features, 0, 0))


def reduce_kernel(
    tm_size, func_size, chunks, norm_count, start_count,
    terms_ref, own_ref, out_ref, loss_ref, every_ref, held_ref, *scratch,
):
    devices = tm_size * func_size
    phases = digits_here(tm_size, func_size)
    count = len(phases)
    landed, sums = scratch[:count], scratch[count : 2 * count]
    small_send, small_recv, send_sem, recv_sem, back_send, back_recv = scratch[2 * count :]
    tm_rank = lax.axis_index("tm")
    me = tm_rank * func_size + lax.axis_index("func")
    barrier = pltpu.get_barrier_semaphore()

    def device_of(other):
        return (other // func_size, lax.rem(other, func_size))

    def greet(step, carry):
        other = lax.rem(me + step, devices)
        pl.semaphore_signal(barrier, inc=1, device_id=device_of(other), device_id_type=MESH_ID)
        return carry

    lax.fori_loop(1, devices, greet, 0)
    every_ref[me] = own_ref[...]
    pl.semaphore_wait(barrier, devices - 1)

    def copy_of(step, slot, other):
        return pltpu.make_async_remote_copy(
            src_ref=own_ref,
            dst_ref=every_ref.at[slot],
            send_sem=small_send.at[step],
            recv_sem=small_recv.at[step],
            device_id=device_of(other),
            device_id_type=MESH_ID,
        )

    def send(step, carry):
        copy_of(step, me, lax.rem(me + step, devices)).start()
        return carry

    def receive(step, carry):
        source = lax.rem(me + devices - step, devices)
        copy = copy_of(step, source, source)
        copy.wait_send()
        copy.wait_recv()
        return carry

    lax.fori_loop(1, devices, send, 0)
    lax.fori_loop(1, devices, receive, 0)
    tiles = []
    for group in range(tm_size):
        tile = every_ref[group * func_size]
        for other in range(1, func_size):
            tile = tile + every_ref[group * func_size + other]
        tiles.append(tile)
    energies = [tile[row : row + 1] / norm_count for tile in tiles for row in range(SLAB_DEV)]
    before, running = [], jnp.zeros_like(energies[0])
    for energy in energies:
        before.append(running)
        running = running + energy
    weighted = jnp.zeros_like(running)
    own_weights = [weighted] * SLAB_DEV
    for spot, energy in enumerate(energies):
        weight = jnp.exp(-causal_rate * before[spot] / (running + epsilon))
        weighted = weighted + weight * energy
        row = spot % SLAB_DEV
        own_weights[row] = jnp.where(tm_rank == spot // SLAB_DEV, weight, own_weights[row])
    start_sum = sum(tile[SLAB_DEV : SLAB_DEV + 1] for tile in tiles)
    loss = weighted / (SLAB_DEV * tm_size) + start_sum / start_count
    loss_ref[...] = jnp.broadcast_to(loss, loss_ref.shape)
    columns = held_ref.shape[1]
    wide = [jnp.concatenate([weight] * (columns // 128), axis=1) for weight in own_weights]
    block = 64

    def combine(step, carry):
        here = pl.ds(pl.multiple_of(step * block, block), block)
        value = terms_ref[SLAB_DEV, here, :]
        for row in range(SLAB_DEV):
            value = value + wide[row] * terms_ref[row, here, :]
        held_ref[here, :] = value
        return carry

    lax.fori_loop(0, held_ref.shape[0] // block, combine, 0)

    copies_each = sum(size - 1 for size, digit, peer_of in phases)

    def total(chunk):
        rows = held_ref.shape[0] // chunks
        begin = chunk * rows
        held, base = held_ref, begin
        begins, sent = [], []
        number = chunk * copies_each
        for spot, (size, digit, peer_of) in enumerate(phases):
            begins.append((begin, rows))
            rows = rows // size
            copies = []
            for step in range(1, size):
                target, device = peer_of(step)
                copy = pltpu.make_async_remote_copy(
                    src_ref=held.at[pl.ds(pl.multiple_of(base + target * rows, 8), rows)],
                    dst_ref=landed[spot].at[chunk, step - 1],
                    send_sem=send_sem.at[number],
                    recv_sem=recv_sem.at[number],
                    device_id=device,
                    device_id_type=MESH_ID,
                )
                copy.start()
                copies.append(copy)
                number += 1
            yield
            value = held[pl.ds(pl.multiple_of(base + digit * rows, 8), rows), :]
            for step, copy in enumerate(copies):
                copy.wait_recv()
                value = value + landed[spot][chunk, step]
            sent.extend(copies)
            begin = begin + digit * rows
            if spot < count - 1:
                sums[spot][chunk] = value
                held, base = sums[spot].at[chunk], 0
            else:
                out_ref[pl.ds(pl.multiple_of(begin, 8), rows), :] = value
        number = chunk * copies_each
        for spot in reversed(range(count)):
            size, digit, peer_of = phases[spot]
            outer, outer_rows = begins[spot]
            width = outer_rows // size
            here = pl.ds(pl.multiple_of(outer + digit * width, 8), width)
            copies = []
            for step in range(1, size):
                copy = pltpu.make_async_remote_copy(
                    src_ref=out_ref.at[here],
                    dst_ref=out_ref.at[here],
                    send_sem=back_send.at[number],
                    recv_sem=back_recv.at[number],
                    device_id=peer_of(step)[1],
                    device_id_type=MESH_ID,
                )
                copy.start()
                sent.append(copy)
                source, device = peer_of(size - step)
                there = pl.ds(pl.multiple_of(outer + source * width, 8), width)
                copies.append(
                    pltpu.make_async_remote_copy(
                        src_ref=out_ref.at[there],
                        dst_ref=out_ref.at[there],
                        send_sem=back_send.at[number],
                        recv_sem=back_recv.at[number],
                        device_id=device,
                        device_id_type=MESH_ID,
                    )
                )
                number += 1
            yield
            for copy in copies:
                copy.wait_recv()
        for copy in sent:
            copy.wait_send()

    running_chunks = [total(chunk) for chunk in range(chunks)]
    while running_chunks:
        running_chunks = [each for each in running_chunks if next(each, True) is None]


def reduce_terms(terms, own, tm_size, func_size, norm_count, start_count):
    groups, total_rows, columns = terms.shape
    devices = tm_size * func_size
    chunks = 4
    while total_rows % (chunks * devices * 8):
        chunks //= 2
    rows = total_rows // chunks
    landed, sums, copies = [], [], 0
    for axis, stride, size in digit_phases(tm_size, func_size):
        rows //= size
        landed.append(pltpu.VMEM((chunks, size - 1, rows, columns), jnp.float32))
        sums.append(pltpu.VMEM((chunks, rows, columns), jnp.float32))
        copies += (size - 1) * chunks
    return pl.pallas_call(
        functools.partial(reduce_kernel, tm_size, func_size, chunks, norm_count, start_count),
        out_shape=(
            jax.ShapeDtypeStruct((total_rows, columns), jnp.float32),
            jax.ShapeDtypeStruct((8, 128), jnp.float32),
        ),
        in_specs=[pl.BlockSpec(memory_space=pltpu.VMEM)] * 2,
        out_specs=[pl.BlockSpec(memory_space=pltpu.VMEM)] * 2,
        scratch_shapes=[
            pltpu.VMEM((devices, 8, 128), jnp.float32),
            pltpu.VMEM((total_rows, columns), jnp.float32),
        ]
        + landed
        + sums
        + [pltpu.SemaphoreType.DMA((devices,))] * 2
        + [pltpu.SemaphoreType.DMA((copies,))] * 4,
        compiler_params=pltpu.CompilerParams(
            collective_id=0, has_side_effects=True, vmem_limit_bytes=vmem_limit
        ),
    )(terms, own)


def local(
    initial_values,
    sensor_columns,
    space_cells,
    time_cells,
    trunk_head,
    trunk_layers,
    trunk_shifts,
    branch_head,
    branch_layers,
    branch_shifts,
):
    time_groups = lax.axis_size("tm")
    func_groups = lax.axis_size("func")
    time_rank = lax.axis_index("tm")
    function_rows, grid_columns = initial_values.shape
    point_rows = space_cells.shape[0]
    breadth = trunk_head.shape[1]
    slab_rows = point_rows // SLAB_DEV
    slab_total = SLAB_DEV * time_groups
    norm_count = function_rows * func_groups * slab_rows
    start_count = function_rows * func_groups * grid_columns
    point_number = jnp.arange(point_rows, dtype=jnp.int32)
    slab_number = (time_rank * SLAB_DEV + point_number // slab_rows).astype(jnp.float32)
    space_points = -1.0 + (2.0 * space_cells.astype(jnp.float32) + 1.0) / grid_columns
    time_points = (slab_number + (time_cells.astype(jnp.float32) + 0.5) / GRID_T) / slab_total
    column_count = grid_columns // time_groups
    column_start = time_rank * column_count
    column_place = (column_start + jnp.arange(column_count, dtype=jnp.int32)).astype(jnp.float32)
    start_space = -1.0 + (2.0 * column_place + 1.0) / grid_columns
    targets = lax.dynamic_slice_in_dim(initial_values, column_start, column_count, 1)
    places = jnp.stack([space_points, time_points], axis=1)
    start_places = jnp.stack([start_space, jnp.zeros_like(start_space)], axis=1)
    depth, branch_depth = trunk_layers.shape[0], branch_layers.shape[0]
    sensors_count = branch_head.shape[0]
    shapes = (
        ("layers", (depth * breadth, breadth)),
        ("branch_layers", (branch_depth * breadth, breadth)),
        ("branch_head", branch_head.shape),
        ("head", trunk_head.shape),
        ("shifts", trunk_shifts.shape),
        ("branch_shifts", branch_shifts.shape),
    )
    used = sum(shape[0] for name, shape in shapes)
    unit = 8 * time_groups * func_groups
    total_rows = used + -used % unit
    stacked = 4 * slab_rows
    half, full = jnp.bfloat16, jnp.float32
    scratch = [
        ((depth, breadth, breadth), half),
        ((depth, breadth, breadth), half),
        ((branch_depth, breadth, breadth), half),
        ((branch_depth, breadth, breadth), half),
        ((depth + 1, stacked, breadth), half),
        ((depth + 1, stacked, breadth), half),
        ((depth, slab_rows, breadth), full),
        ((depth - 1, stacked, breadth), full),
        ((branch_depth, function_rows, breadth), full),
        ((branch_depth, function_rows, breadth), half),
        ((branch_depth, function_rows, breadth), half),
        ((function_rows, sensors_count), half),
        ((function_rows, sensors_count), half),
        ((function_rows, breadth), half),
        ((function_rows, breadth), half),
    ]
    terms, own = pl.pallas_call(
        functools.partial(terms_kernel, 2.0 / (norm_count * slab_total), 2.0 / start_count),
        out_shape=(
            jax.ShapeDtypeStruct((SLAB_DEV + 1, total_rows, breadth), jnp.float32),
            jax.ShapeDtypeStruct((8, 128), jnp.float32),
        ),
        in_specs=[pl.BlockSpec(memory_space=pltpu.VMEM)] * 11,
        out_specs=[pl.BlockSpec(memory_space=pltpu.VMEM)] * 2,
        scratch_shapes=[pltpu.VMEM(shape, kind) for shape, kind in scratch],
        compiler_params=pltpu.CompilerParams(vmem_limit_bytes=vmem_limit),
    )(
        initial_values,
        targets,
        sensor_columns.reshape(1, sensors_count),
        places,
        start_places,
        trunk_head,
        trunk_layers,
        trunk_shifts,
        branch_head,
        branch_layers,
        branch_shifts,
    )
    packed, loss = reduce_terms(terms, own, time_groups, func_groups, norm_count, start_count)
    summed, begin = {}, 0
    for name, shape in shapes:
        summed[name] = packed[begin : begin + shape[0]]
        begin += shape[0]
    return (
        loss[0, 0:1],
        summed["head"],
        summed["layers"].reshape(trunk_layers.shape),
        summed["shifts"],
        summed["branch_head"],
        summed["branch_layers"].reshape(branch_layers.shape),
        summed["branch_shifts"],
    )


def solution(mesh):
    in_specs = (P("func", None), P(), P("tm"), P("tm"), P(), P(), P(), P(), P(), P())
    out_specs = (P(), P(), P(), P(), P(), P(), P())
    return jax.shard_map(local, mesh=mesh, in_specs=in_specs, out_specs=out_specs, check_vma=False)
```

profile of v0, /device:TPU:0, one launch (start us, length us, event | category | flops | bytes accessed | tf_op | source)
XLA Modules:
  0.0 106.3 jit_solution(1066391833310829771)
XLA Ops:
  0.6 0.7 fusion.3
  1.3 0.7 multiply_add_fusion.1
  2.0 1.5 %constant_dynamic-slice_fusion.target_ref = f32[128,128]{1,0:T(8,128)} fusion(f32[128,1024]{1,0:T(8,128)} %initial_ref.1, s32[]{:T(128)S(6)} %select_n.8), kind=kLoop, calls=%fused_computation.14 | loop fusion | bytes 131076 | tf_op jit(solution)/shard_map/dynamic_slice | solution.py:527
  3.5 0.6 stack.16.start_ref
  4.2 0.9 copy.21.place_ref
  5.0 35.4 %shard_map.153 = (f32[5,2048,256]{2,1,0:T(8,128)}, f32[8,128]{1,0:T(8,128)}) custom-call(f32[128,1024]{1,0:T(8,128)} %initial_ref.1, f32[128,128]{1,0:T(8,128)} %constant_dynamic-slice_fusion.target_ref, s32[1,128]{1,0:T(1,128)} %bitcast.10, f32[512,2]{1,0:T(8,128)} %copy.21.place_ref, f32[128,2]{1,0:T(8,128)} %stack.16.start_ref, f32[2,256]{1,0:T(2,128)} %head_ref.1, ...), custom_call_target="tpu_custom_call" | custom-call | tf_op jit(solution)/shard_map/pallas_call | solution.py:562
  40.5 54.8 %shard_map.154 = (f32[2048,256]{1,0:T(8,128)}, f32[8,128]{1,0:T(8,128)}) custom-call(f32[5,2048,256]{2,1,0:T(8,128)} %get-tuple-element.11.terms_ref, f32[8,128]{1,0:T(8,128)} %get-tuple-element.12.own_ref), custom_call_target="tpu_custom_call" | custom-call | tf_op jit(solution)/shard_map/pallas_call | solution.py:475
  95.3 1.2 %slice.21 = f32[1,1]{1,0:T(1,128)} slice(f32[8,128]{1,0:T(8,128)} %get-tuple-element.13), slice={[0:1], [0:1]} | slice | bytes 8 | tf_op jit(solution)/shard_map/slice | solution.py:591
  96.5 1.3 %slice.22 = f32[2,256]{1,0:T(2,128)} slice(f32[2048,256]{1,0:T(8,128)} %get-tuple-element.14), slice={[1920:1922], [0:256]} | slice | bytes 4096 | tf_op jit(solution)/shard_map/slice | solution.py:588
  97.8 1.3 %slice.24 = f32[4,256]{1,0:T(4,128)} slice(f32[2048,256]{1,0:T(8,128)} %get-tuple-element.14), slice={[1922:1926], [0:256]} | slice | bytes 8192 | tf_op jit(solution)/shard_map/slice | solution.py:588
  99.1 1.3 %slice.27 = f32[5,256]{1,0:T(8,128)} slice(f32[2048,256]{1,0:T(8,128)} %get-tuple-element.14), slice={[1926:1931], [0:256]} | slice | bytes 10240 | tf_op jit(solution)/shard_map/slice | solution.py:588
  100.4 1.6 %slice.25 = f32[128,256]{1,0:T(8,128)} slice(f32[2048,256]{1,0:T(8,128)} %get-tuple-element.14), slice={[1792:1920], [0:256]} | slice | bytes 262144 | tf_op jit(solution)/shard_map/slice | solution.py:588
  102.0 2.1 %slice.23 = f32[768,256]{1,0:T(8,128)} slice(f32[2048,256]{1,0:T(8,128)} %get-tuple-element.14), slice={[0:768], [0:256]} | slice | bytes 1572864 | tf_op jit(solution)/shard_map/slice | solution.py:588
  104.0 2.3 %slice.26 = f32[1024,256]{1,0:T(8,128)} slice(f32[2048,256]{1,0:T(8,128)} %get-tuple-element.14), slice={[768:1792], [0:256]} | slice | bytes 2097152 | tf_op jit(solution)/shard_map/slice | solution.py:588
  (2 shorter events, 0.0 us)
where the time goes:
time: 107 us; the launch traced here: 106 us
  Pallas kernels  90.3 us (84%)
  local copies, waits for them, and re-layouts  13.9 us (13%)
  other arithmetic  1.41 us (1%)
    pallas_call x1, Pallas kernels, reduce_terms(): pl.pallas_call(functools.partial(reduce_kernel, tm_size, func_size, chunk...  54.8 us
    pallas_call x1, Pallas kernels, local(): pl.pallas_call(functools.partial(terms_kernel, 2.0 / (norm_count * slab_t...  35.4 us
    slice x6, local copies, waits for them, and re-layouts, local(): summed[name] = packed[begin:begin + shape[0]]  9.77 us

commit v1 on v0

--- a/solution.py
+++ b/solution.py
@@ -492,6 +492,19 @@
             collective_id=0, has_side_effects=True, vmem_limit_bytes=vmem_limit
         ),
     )(terms, own)
+
+
+def unpack_kernel(packed_ref, *out_refs):
+    begin = 0
+    for out_ref in out_refs:
+        rows = out_ref.shape[-2]
+        if len(out_ref.shape) == 3:
+            for layer in range(out_ref.shape[0]):
+                out_ref[layer] = packed_ref[begin : begin + rows, :]
+                begin += rows
+        else:
+            out_ref[...] = packed_ref[begin : begin + rows, :]
+            begin += rows
 
 
 def local(
@@ -583,19 +596,15 @@
         branch_shifts,
     )
     packed, loss = reduce_terms(terms, own, time_groups, func_groups, norm_count, start_count)
-    summed, begin = {}, 0
-    for name, shape in shapes:
-        summed[name] = packed[begin : begin + shape[0]]
-        begin += shape[0]
-    return (
-        loss[0, 0:1],
-        summed["head"],
-        summed["layers"].reshape(trunk_layers.shape),
-        summed["shifts"],
-        summed["branch_head"],
-        summed["branch_layers"].reshape(branch_layers.shape),
-        summed["branch_shifts"],
-    )
+    parts = (trunk_layers, branch_layers, branch_head, trunk_head, trunk_shifts, branch_shifts)
+    layers, branch, first, head, shifts, offsets = pl.pallas_call(
+        unpack_kernel,
+        out_shape=tuple(jax.ShapeDtypeStruct(part.shape, jnp.float32) for part in parts),
+        in_specs=[pl.BlockSpec(memory_space=pltpu.VMEM)],
+        out_specs=[pl.BlockSpec(memory_space=pltpu.VMEM)] * 6,
+        compiler_params=pltpu.CompilerParams(vmem_limit_bytes=vmem_limit // 4),
+    )(packed)
+    return (loss[0, 0:1], head, layers, shifts, first, branch, offsets)
 
 
 def solution(mesh):

time: 107 us -> 99.8 us (0.933)
  local copies, waits for them, and re-layouts: 13.9 us -> 5.75 us
  Pallas kernels: 90.3 us -> 91.7 us
    slice x7 -> x1, local copies, waits for them, and re-layouts: 11 us -> 1.19 us  [local(): return (loss[0, 0:1], head, layers, shifts, first, branch, offsets)]
    unnamed x0 -> x2, local copies, waits for them, and re-layouts: none -> 1.59 us
    pallas_call x0 -> x1, Pallas kernels: none -> 1.39 us  [local(): pl.pallas_call(unpack_kernel, out_shape=tuple((jax.ShapeDtypeStruct(part....]
where the time goes in v1:
time: 99.8 us; the launch traced here: 99.5 us
  Pallas kernels  91.7 us (92%)
  local copies, waits for them, and re-layouts  5.75 us (6%)
  other arithmetic  1.41 us (1%)
    pallas_call x1, Pallas kernels, reduce_terms(): pl.pallas_call(functools.partial(reduce_kernel, tm_size, func_size, chunk...  54.8 us
    pallas_call x1, Pallas kernels, local(): pl.pallas_call(functools.partial(terms_kernel, 2.0 / (norm_count * slab_t...  35.4 us

profile of v1, /device:TPU:0, one launch (start us, length us, event | category | flops | bytes accessed | tf_op | source)
XLA Modules:
  0.0 99.5 jit_solution(7418588698602648134)
XLA Ops:
  0.6 0.7 fusion.3
  1.3 0.7 multiply_add_fusion.1
  2.0 1.5 %constant_dynamic-slice_fusion.target_ref = f32[128,128]{1,0:T(8,128)} fusion(f32[128,1024]{1,0:T(8,128)} %initial_ref.1, s32[]{:T(128)S(6)} %select_n.8), kind=kLoop, calls=%fused_computation.14 | loop fusion | bytes 131076 | tf_op jit(solution)/shard_map/dynamic_slice | solution.py:540
  3.5 0.6 stack.16.start_ref
  4.2 0.9 copy.21.place_ref
  5.0 35.4 %shard_map.153 = (f32[5,2048,256]{2,1,0:T(8,128)}, f32[8,128]{1,0:T(8,128)}) custom-call(f32[128,1024]{1,0:T(8,128)} %initial_ref.1, f32[128,128]{1,0:T(8,128)} %constant_dynamic-slice_fusion.target_ref, s32[1,128]{1,0:T(1,128)} %bitcast.6, f32[512,2]{1,0:T(8,128)} %copy.21.place_ref, f32[128,2]{1,0:T(8,128)} %stack.16.start_ref, f32[2,256]{1,0:T(2,128)} %head_ref.1, ...), custom_call_target="tpu_custom_call" | custom-call | tf_op jit(solution)/shard_map/pallas_call | solution.py:575
  40.5 54.8 %shard_map.154 = (f32[2048,256]{1,0:T(8,128)}, f32[8,128]{1,0:T(8,128)}) custom-call(f32[5,2048,256]{2,1,0:T(8,128)} %get-tuple-element.17.terms_ref, f32[8,128]{1,0:T(8,128)} %get-tuple-element.18.own_ref), custom_call_target="tpu_custom_call" | custom-call | tf_op jit(solution)/shard_map/pallas_call | solution.py:475
  95.3 1.2 %slice.3 = f32[1,1]{1,0:T(1,128)} slice(f32[8,128]{1,0:T(8,128)} %get-tuple-element.19), slice={[0:1], [0:1]} | slice | bytes 8 | tf_op jit(solution)/shard_map/slice | solution.py:607
  96.5 0.0 copy-start
  96.5 1.6 %copy-done = f32[2048,256]{1,0:T(8,128)S(1)} copy-done((f32[2048,256]{1,0:T(8,128)S(1)}, f32[2048,256]{1,0:T(8,128)}, u32[]{:S(2)}) %copy-start) | copy-done | bytes 2097176
  98.1 1.4 %shard_map.155 = (f32[3,256,256]{2,1,0:T(8,128)}, f32[4,256,256]{2,1,0:T(8,128)}, f32[128,256]{1,0:T(8,128)}, f32[2,256]{1,0:T(2,128)}, f32[4,256]{1,0:T(4,128)}, /*index=5*/f32[5,256]{1,0:T(8,128)}) custom-call(f32[2048,256]{1,0:T(8,128)S(1)} %copy-done), custom_call_target="tpu_custom_call" | custom-call | tf_op jit(solution)/shard_map/pallas_call | solution.py:600
  (2 shorter events, 0.0 us)
Async XLA Ops:
  96.5 1.6 %copy-start = (f32[2048,256]{1,0:T(8,128)S(1)}, f32[2048,256]{1,0:T(8,128)}, u32[]{:S(2)}) copy-start(f32[2048,256]{1,0:T(8,128)} %get-tuple-element.20.packed_ref) | copy-start | bytes 6291460
